TPU v7x, 32 devices: a whole 2x2x4 slice. The times are simulated.
32 devices in a mesh: dp: 4 (over x, core), half: 2 (over y), own: 4 (over z).
Axes of the slice: x: 2, y: 2, z: 4, core: 2. Of those that a mesh axis runs over, the one named last changes fastest.
Arguments:
- grad_parts: bfloat16 [4, 6, 1024, 1024], P('dp', None, ('half', 'own')), may hold values from -6 to 6
- owner_table: int32 [6, 1], replicated, may hold values from 0 to 3; in each aligned block of 6 rows (0 to 5, 6 to 11, ...) at most 2 rows name the same one
- left_basis: bfloat16 [8, 1024, 1024], P(('half', 'own')), may hold values from -0.1875 to 0.1875
- right_basis: bfloat16 [8, 1024, 1024], P(('half', 'own')), may hold values from -0.1875 to 0.1875
- first_moment: bfloat16 [8, 1024, 1024], P(('half', 'own'), 'dp'), may hold values from -6 to 6
- second_moment: bfloat16 [8, 1024, 1024], P(('half', 'own'), 'dp'), may hold values from 0.5 to 8
Outputs:
- update: bfloat16 [6, 1024, 1024], P(None, ('half', 'own'), 'dp')
Inputs may be any that keep to these rules, and one draw needn't show every extreme that they name: `owner_table`: every owner index is named by at least one block and by at most 2 blocks; some owner is named by exactly 2 blocks.
All inputs are finite; a program needn't handle non-finite values.
Results may differ from a plain program's by a relative error of at most 0.013.
Values may be sent and summed in bfloat16 or wider, within the bound.
A program may use at most 128 MiB of HBM per device.

v0:
```python
import jax
import jax.numpy as jnp
from jax import lax
from jax.sharding import PartitionSpec as P

beta_first = 0.9
beta_second = 0.95
bias_first = 1.0 - 0.9**10
bias_second = 1.0 - 0.95**10
epsilon = 1e-08


def slot_select(owner_table, owner_count, slot_count):
    owner_ids = owner_table[:, 0]
    positions = jnp.arange(owner_ids.shape[0], dtype=jnp.int32)
    shared = (owner_ids[:, None] == owner_ids[None, :]) & (positions[None, :] < positions[:, None])
    ranking = jnp.sum(shared.astype(jnp.int32), axis=1)
    slot_ids = ranking * owner_count + owner_ids
    slot_range = jnp.arange(slot_count, dtype=jnp.int32)
    return (slot_range[:, None] == slot_ids[None, :]).astype(jnp.bfloat16)


def local(grad_parts, owner_table, left_basis, right_basis, first_moment, second_moment):
    halves = lax.axis_size("half")
    owners = lax.axis_size("own")
    replicas = lax.axis_size("dp")
    block_count = grad_parts.shape[1]
    piece_rows = grad_parts.shape[2]
    block_width = grad_parts.shape[3]
    quarter = block_width // replicas
    offset = lax.axis_index("dp") * quarter
    summed = lax.psum_scatter(
        grad_parts[0].astype(jnp.float32).astype(jnp.bfloat16),
        "dp",
        scatter_dimension=2,
        tiled=True,
    )
    selector = slot_select(owner_table, owners, halves * owners)
    flat_grad = summed.reshape(block_count, piece_rows * quarter)
    packed = jnp.dot(selector, flat_grad, preferred_element_type=jnp.float32).astype(jnp.bfloat16)
    packed = packed.reshape(halves, owners, piece_rows, quarter)
    arrived = lax.all_to_all(
        lax.all_to_all(packed, "half", split_axis=0, concat_axis=0, tiled=True),
        "own",
        split_axis=1,
        concat_axis=1,
        tiled=True,
    )
    grad_block = arrived.reshape(block_width, quarter)
    left_matrix = left_basis[0]
    right_matrix = right_basis[0]
    right_rows = lax.dynamic_slice_in_dim(right_matrix, offset, quarter, 0)
    left_slice = lax.dynamic_slice_in_dim(left_matrix, offset, quarter, 1)
    projected = lax.dot_general(
        left_slice,
        lax.all_gather(grad_block, "dp", axis=1, tiled=True),
        (((0,), (0,)), ((), ())),
        preferred_element_type=jnp.float32,
    )
    rotated = jnp.dot(
        projected.astype(jnp.bfloat16), right_matrix, preferred_element_type=jnp.float32
    )
    first_new = beta_first * first_moment[0].astype(jnp.float32) + (1.0 - beta_first) * rotated
    second_new = (
        beta_second * second_moment[0].astype(jnp.float32) + (1.0 - beta_second) * rotated * rotated
    )
    direction = (first_new / bias_first / (jnp.sqrt(second_new / bias_second) + epsilon)).astype(
        jnp.bfloat16
    )
    partial_cols = lax.dot_general(
        lax.all_gather(direction, "dp", axis=0, tiled=True),
        right_rows,
        (((1,), (1,)), ((), ())),
        preferred_element_type=jnp.float32,
    )
    update_block = jnp.dot(
        left_matrix, partial_cols.astype(jnp.bfloat16), preferred_element_type=jnp.float32
    )
    outgoing = update_block.astype(jnp.bfloat16).reshape(halves, owners, piece_rows, quarter)
    returned = lax.all_to_all(
        lax.all_to_all(outgoing, "half", split_axis=0, concat_axis=0, tiled=True),
        "own",
        split_axis=1,
        concat_axis=1,
        tiled=True,
    )
    flat_back = returned.reshape(halves * owners, piece_rows * quarter)
    placed = lax.dot_general(
        selector, flat_back, (((0,), (0,)), ((), ())), preferred_element_type=jnp.float32
    )
    return placed.astype(jnp.bfloat16).reshape(block_count, piece_rows, quarter)


def solution(mesh):
    return jax.shard_map(
        local,
        mesh=mesh,
        in_specs=(
            P("dp", None, ("half", "own"), None),
            P(),
            P(("half", "own"), None, None),
            P(("half", "own"), None, None),
            P(("half", "own"), "dp", None),
            P(("half", "own"), "dp", None),
        ),
        out_specs=P(None, ("half", "own"), "dp"),
        check_vma=False,
    )
```

profile of v0, /device:TPU:0, one launch (start us, length us, event | category | flops | bytes accessed | tf_op | source)
XLA Modules:
  0.0 161.1 jit_solution(16821739264425904918)
XLA Ops:
  6.5 0.0 copy-start
  6.5 0.0 reduce-scatter.2.cloned.1.call-start
  6.5 0.7 reduce-scatter.2.cloned.1.call-update
  7.3 0.0 all-gather.3.cloned.1.call-start
  7.3 0.9 convert_reduce_fusion
  8.2 0.7 multiply_add_fusion
  8.9 31.8 %reduce-scatter.2.cloned.1.call-done = bf16[6,128,256]{2,1,0:T(8,128)(2,1)} async-done(((bf16[6,128,1024]{2,1,0:T(8,128)(2,1)}), bf16[6,128,256]{2,1,0:T(8,128)(2,1)}) %reduce-scatter.2.cloned.1.call-update) | async-done | bytes 393232 | tf_op jit(solution)/shard_map/reduce_scatter | solution.py:32
  40.7 1.2 copy.26
  41.9 0.3 convolution_convert_fusion.1
  42.2 0.1 copy.27
  42.3 10.5 %all_to_all.20 = bf16[2,4,128,256]{3,2,1,0:T(8,128)(2,1)S(1)} all-to-all(bf16[2,4,128,256]{3,2,1,0:T(8,128)(2,1)S(1)} %bitcast.60), channel_id=1, replica_groups=mesh['dp'=4,'half'=2,'own'=4] {'half'}, dimensions={0} | all-to-all | bytes 1048576 | tf_op jit(solution)/shard_map/all_to_all | solution.py:43
  52.8 0.0 copy-start.1
  52.8 0.0 copy-start.2
  52.8 17.9 %all_to_all.21 = bf16[2,4,128,256]{3,2,0,1:T(8,128)(2,1)S(1)} all-to-all(bf16[2,4,128,256]{3,2,0,1:T(8,128)(2,1)S(1)} %copy.20), channel_id=1, replica_groups=mesh['dp'=4,'half'=2,'own'=4] {'own'}, dimensions={1} | all-to-all | bytes 1048576 | tf_op jit(solution)/shard_map/all_to_all | solution.py:42
  70.7 0.8 copy.21
  71.6 0.0 all-gather.3.cloned.1.call-update
  71.6 0.0 all-gather.5.cloned.1.call-start
  71.6 20.2 %all-gather.3.cloned.1.call-done = bf16[1024,1024]{1,0:T(8,128)(2,1)} async-done(((bf16[1024,256]{1,0:T(8,128)(2,1)}), bf16[1024,1024]{1,0:T(8,128)(2,1)}) %all-gather.3.cloned.1.call-update) | async-done | bytes 2097168 | tf_op jit(solution)/shard_map/all_gather | solution.py:56
  91.8 0.0 copy-done
  91.8 0.0 copy-done.1
  91.8 0.0 copy-done.2
  91.8 5.0 %fusion.16 = bf16[256,1024]{1,0:T(8,128)(2,1)} fusion(bf16[1,256,1024]{2,1,0:T(8,128)(2,1)S(1)} %copy-done.1, bf16[1,256,1024]{2,1,0:T(8,128)(2,1)S(1)} %copy-done.2, bf16[1,1024,1024]{2,1,0:T(8,128)(2,1)} %param.9, bf16[1024,1024]{1,0:T(8,128)(2,1)} %all-gather.3.cloned.1.call-done, bf16[1,1024,1024]{2,1,0:T(8,128)(2,1)S(1)} %copy-done, s32[]{:T(128)S(6)} %select_n.4), kind=kOutput, calls=%fused_computation.18 | convolution fusion | flops 1077673984 | bytes 6291460 | tf_op jit(solution)/shard_map/dot_general | solution.py:60
  96.8 0.0 all-gather.5.cloned.1.call-update
  96.8 22.7 %all-gather.5.cloned.1.call-done = bf16[1024,1024]{1,0:T(8,128)(2,1)} async-done(((bf16[256,1024]{1,0:T(8,128)(2,1)}), bf16[1024,1024]{1,0:T(8,128)(2,1)}) %all-gather.5.cloned.1.call-update) | async-done | bytes 2097168 | tf_op jit(solution)/shard_map/all_gather | solution.py:71
  119.5 4.0 %fusion.7 = bf16[1024,256]{0,1:T(8,128)(2,1)S(1)} fusion(bf16[1,1024,1024]{2,1,0:T(8,128)(2,1)S(1)} %copy-done, bf16[1024,1024]{1,0:T(8,128)(2,1)} %all-gather.5.cloned.1.call-done, bf16[1,1024,1024]{2,1,0:T(8,128)(2,1)} %param.9, s32[]{:T(128)S(6)} %select_n.4), kind=kOutput, calls=%fused_computation.10 | convolution fusion | flops 1074266112 | bytes 5242884 | tf_op jit(solution)/shard_map/dot_general | solution.py:76
  123.5 0.2 copy.25
  123.7 11.1 %all_to_all.22 = bf16[2,4,128,256]{3,2,1,0:T(8,128)(2,1)S(1)} all-to-all(bf16[2,4,128,256]{3,2,1,0:T(8,128)(2,1)S(1)} %bitcast.61), channel_id=1, replica_groups=mesh['dp'=4,'half'=2,'own'=4] {'half'}, dimensions={0} | all-to-all | bytes 1048576 | tf_op jit(solution)/shard_map/all_to_all | solution.py:81
  134.8 18.3 %all_to_all.23 = bf16[2,4,128,256]{3,2,0,1:T(8,128)(2,1)S(1)} all-to-all(bf16[2,4,128,256]{3,2,0,1:T(8,128)(2,1)S(1)} %copy.23), channel_id=1, replica_groups=mesh['dp'=4,'half'=2,'own'=4] {'own'}, dimensions={1} | all-to-all | bytes 1048576 | tf_op jit(solution)/shard_map/all_to_all | solution.py:80
  153.1 0.3 copy.28
  153.4 0.4 convolution_convert_fusion
  153.8 0.8 copy.31
  (3 shorter events, 0.1 us)
Async XLA Ops:
  6.5 85.3 %copy-start = (bf16[1,1024,1024]{2,1,0:T(8,128)(2,1)S(1)}, bf16[1,1024,1024]{2,1,0:T(8,128)(2,1)}, u32[]{:S(2)}) copy-start(bf16[1,1024,1024]{2,1,0:T(8,128)(2,1)} %param.8) | copy-start | bytes 6291460
  6.5 34.1 %reduce-scatter.2.cloned.1.call-start = ((), (), s32[]{:S(2)}) async-start(), calls=%async_computation.5 | async-start | bytes 1966080 | tf_op jit(solution)/shard_map/reduce_scatter | solution.py:32
  7.3 84.6 %all-gather.3.cloned.1.call-start = ((), (), s32[]{:S(2)}) async-start(), calls=%async_computation.6 | async-start | bytes 2621440 | tf_op jit(solution)/shard_map/all_gather | solution.py:56
  52.8 39.0 %copy-start.1 = (bf16[1,256,1024]{2,1,0:T(8,128)(2,1)S(1)}, bf16[1,256,1024]{2,1,0:T(8,128)(2,1)}, u32[]{:S(2)}) copy-start(bf16[1,256,1024]{2,1,0:T(8,128)(2,1)} %param.11) | copy-start | bytes 1572868
  52.8 39.0 %copy-start.2 = (bf16[1,256,1024]{2,1,0:T(8,128)(2,1)S(1)}, bf16[1,256,1024]{2,1,0:T(8,128)(2,1)}, u32[]{:S(2)}) copy-start(bf16[1,256,1024]{2,1,0:T(8,128)(2,1)} %param.10) | copy-start | bytes 1572868
  71.6 47.9 %all-gather.5.cloned.1.call-start = ((), (), s32[]{:S(2)}) async-start(), calls=%async_computation.7 | async-start | bytes 2621440 | tf_op jit(solution)/shard_map/all_gather | solution.py:71
Sparse Core Ops, SparseCore 0:
  9.9 30.7 reduce-scatter.1
  71.7 20.0 all-gather.2
  96.9 22.5 all-gather.4
where the time goes:
time: 162 us; the launch traced here: 161 us
  waiting for transfers between devices  75.4 us (47%)
  blocking collectives  57.7 us (36%)
  between operations  13.2 us (8%)
  matrix products  9.55 us (6%)
  local copies, waits for them, and re-layouts  3.59 us (2%)
    reduce_scatter x1, waiting for transfers between devices, local(): lax.psum_scatter(grad_parts[0].astype(jnp.float32).astype(jnp.bfloat16),...  31.8 us
    all_gather x1, waiting for transfers between devices, local(): lax.all_gather(direction, 'dp', axis=0, tiled=True)  22.7 us
    all_gather x1, waiting for transfers between devices, local(): lax.all_gather(grad_block, 'dp', axis=1, tiled=True)  20.2 us
    all_to_all x1, blocking collectives, local(): lax.all_to_all(lax.all_to_all(outgoing, 'half', split_axis=0, concat_axis...  18.3 us
    all_to_all x1, blocking collectives, local(): lax.all_to_all(lax.all_to_all(packed, 'half', split_axis=0, concat_axis=0...  17.9 us
    all_to_all x1, blocking collectives, local(): lax.all_to_all(outgoing, 'half', split_axis=0, concat_axis=0, tiled=True)  11.1 us
    all_to_all x1, blocking collectives, local(): lax.all_to_all(packed, 'half', split_axis=0, concat_axis=0, tiled=True)  10.5 us
    dot_general x1, matrix products, local(): jnp.dot(projected.astype(jnp.bfloat16), right_matrix, preferred_element_t...  4.95 us
  transfers between devices with their start and end apart: 3, of which 3 were waited for; matrix products, arithmetic and copies ran while one was open for 1% of the time, Pallas kernels for 0%

commit v1 on v0

--- a/solution.py
+++ b/solution.py
@@ -8,6 +8,18 @@
 bias_first = 1.0 - 0.9**10
 bias_second = 1.0 - 0.95**10
 epsilon = 1e-08
+
+
+def doubled_up(x, axis, dim):
+    ways, here, step = (lax.axis_size(axis), lax.axis_index(axis), x.shape[dim])
+    line, have = (x, 1)
+    while have < ways:
+        line = jnp.concatenate(
+            [line, lax.ppermute(line, axis, [(d, (d - have) % ways) for d in range(ways)])],
+            axis=dim,
+        )
+        have = 2 * have
+    return jnp.roll(line, here * step, axis=dim)
 
 
 def slot_select(owner_table, owner_count, slot_count):
@@ -68,7 +80,7 @@
         jnp.bfloat16
     )
     partial_cols = lax.dot_general(
-        lax.all_gather(direction, "dp", axis=0, tiled=True),
+        doubled_up(direction, "dp", 0),
         right_rows,
         (((1,), (1,)), ((), ())),
         preferred_element_type=jnp.float32,

time: 162 us -> 180 us (1.11)
  local copies, waits for them, and re-layouts: 3.59 us -> 10.6 us
  waiting for transfers between devices: 75.4 us -> 82.3 us
  starting transfers between devices: 0.08 us -> 1.93 us
    ppermute x0 -> x2, waiting for transfers between devices: none -> 29.5 us  [doubled_up(): lax.ppermute(line, axis, [(d, (d - have) % ways) for d in range(ways)])]
    all_gather x1 -> x0, waiting for transfers between devices: 22.7 us -> none  [local(): lax.all_gather(direction, 'dp', axis=0, tiled=True)]
    unnamed x10 -> x12, local copies, waits for them, and re-layouts: 2.45 us -> 7.24 us
    concatenate x0 -> x1, local copies, waits for them, and re-layouts: none -> 2.27 us  [doubled_up(): return jnp.roll(line, here * step, axis=dim)]
    ppermute x0 -> x2, starting transfers between devices: none -> 1.89 us  [doubled_up(): lax.ppermute(line, axis, [(d, (d - have) % ways) for d in range(ways)])]
  transfers between devices with their start and end apart: 3 -> 4, of which waited for: 3 -> 4; matrix products, arithmetic and copies ran while one was open for 1% -> 1% of each run, Pallas kernels for 0% -> 0%
where the time goes in v1:
time: 180 us; the launch traced here: 179 us
  waiting for transfers between devices  82.3 us (46%)
  blocking collectives  58.9 us (33%)
  between operations  13.5 us (8%)
  local copies, waits for them, and re-layouts  10.6 us (6%)
  matrix products  9.61 us (5%)
  other arithmetic  2.65 us (1%)
  starting transfers between devices  1.93 us (1%)
    reduce_scatter x1, waiting for transfers between devices, local(): lax.psum_scatter(grad_parts[0].astype(jnp.float32).astype(jnp.bfloat16),...  31.8 us
    ppermute x2, waiting for transfers between devices, doubled_up(): lax.ppermute(line, axis, [(d, (d - have) % ways) for d in range(ways)])  29.5 us
    all_gather x1, waiting for transfers between devices, local(): lax.all_gather(grad_block, 'dp', axis=1, tiled=True)  20.2 us
    all_to_all x1, blocking collectives, local(): lax.all_to_all(lax.all_to_all(outgoing, 'half', split_axis=0, concat_axis...  18.8 us
    all_to_all x1, blocking collectives, local(): lax.all_to_all(lax.all_to_all(packed, 'half', split_axis=0, concat_axis=0...  17.9 us
    all_to_all x1, blocking collectives, local(): lax.all_to_all(outgoing, 'half', split_axis=0, concat_axis=0, tiled=True)  11.7 us
    all_to_all x1, blocking collectives, local(): lax.all_to_all(packed, 'half', split_axis=0, concat_axis=0, tiled=True)  10.5 us
    unnamed x12, local copies, waits for them, and re-layouts  7.24 us
  transfers between devices with their start and end apart: 4, of which 4 were waited for; matrix products, arithmetic and copies ran while one was open for 1% of the time, Pallas kernels for 0%

profile of v1, /device:TPU:0, one launch (start us, length us, event | category | flops | bytes accessed | tf_op | source)
XLA Modules:
  0.0 179.5 jit_solution(849044435299132783)
XLA Ops:
  6.5 0.7 reduce-scatter.2.cloned.1.call-update
  7.3 0.0 all-gather.2.cloned.1.call-start
  7.3 0.9 convert_reduce_fusion
  8.2 0.7 multiply_add_fusion
  8.9 31.8 %reduce-scatter.2.cloned.1.call-done = bf16[6,128,256]{2,1,0:T(8,128)(2,1)} async-done(((bf16[6,128,1024]{2,1,0:T(8,128)(2,1)}), bf16[6,128,256]{2,1,0:T(8,128)(2,1)}) %reduce-scatter.2.cloned.1.call-update) | async-done | bytes 393232 | tf_op jit(solution)/shard_map/reduce_scatter | solution.py:44
  40.7 1.2 copy.26
  41.9 0.3 convolution_convert_fusion.1
  42.2 0.1 copy.27
  42.3 10.5 %all_to_all.20 = bf16[2,4,128,256]{3,2,1,0:T(8,128)(2,1)S(1)} all-to-all(bf16[2,4,128,256]{3,2,1,0:T(8,128)(2,1)S(1)} %bitcast.63), channel_id=1, replica_groups=mesh['dp'=4,'half'=2,'own'=4] {'half'}, dimensions={0} | all-to-all | bytes 1048576 | tf_op jit(solution)/shard_map/all_to_all | solution.py:55
  52.8 17.9 %all_to_all.21 = bf16[2,4,128,256]{3,2,0,1:T(8,128)(2,1)S(1)} all-to-all(bf16[2,4,128,256]{3,2,0,1:T(8,128)(2,1)S(1)} %copy.20), channel_id=1, replica_groups=mesh['dp'=4,'half'=2,'own'=4] {'own'}, dimensions={1} | all-to-all | bytes 1048576 | tf_op jit(solution)/shard_map/all_to_all | solution.py:54
  70.7 0.8 copy.21
  71.5 0.0 all-gather.2.cloned.1.call-update
  71.6 20.2 %all-gather.2.cloned.1.call-done = bf16[1024,1024]{1,0:T(8,128)(2,1)} async-done(((bf16[1024,256]{1,0:T(8,128)(2,1)}), bf16[1024,1024]{1,0:T(8,128)(2,1)}) %all-gather.2.cloned.1.call-update) | async-done | bytes 2097168 | tf_op jit(solution)/shard_map/all_gather | solution.py:68
  91.8 0.0 copy-done.1
  91.8 5.0 %constant_dynamic-update-slice_fusion.5 = (bf16[2048,1024]{1,0:T(8,128)(2,1)}, bf16[256,1024]{1,0:T(8,128)(2,1)S(1)}) fusion(bf16[1,256,1024]{2,1,0:T(8,128)(2,1)S(1)} %copy-done.1, bf16[1,1024,1024]{2,1,0:T(8,128)(2,1)} %param.9, bf16[1024,1024]{1,0:T(8,128)(2,1)} %all-gather.2.cloned.1.call-done, bf16[1,1024,1024]{2,1,0:T(8,128)(2,1)S(1)} %copy-done, ...), kind=kOutput, calls=%fused_computation.32 | convolution fusion | flops 1077673984 | bytes 6815748 | tf_op jit(solution)/shard_map/dot_general | solution.py:72
  96.8 0.2 collective-permute-start
  97.0 6.7 %collective-permute-done = bf16[256,1024]{1,0:T(8,128)(2,1)S(1)} collective-permute-done((bf16[256,1024]{1,0:T(8,128)(2,1)S(1)}, bf16[256,1024]{1,0:T(8,128)(2,1)S(1)}, u32[]{:S(2)}, u32[]{:S(2)}) %collective-permute-start) | collective-permute-done | bytes 524320 | tf_op jit(solution)/shard_map/ppermute | solution.py:18
  103.7 1.1 pad_maximum_fusion
  104.8 1.7 collective-permute-start.1
  106.5 0.8 constant_dynamic-update-slice_fusion.4
  107.3 22.8 %collective-permute-done.1 = bf16[512,1024]{1,0:T(8,128)(2,1)} collective-permute-done((bf16[512,1024]{1,0:T(8,128)(2,1)}, bf16[512,1024]{1,0:T(8,128)(2,1)}, u32[]{:S(2)}, u32[]{:S(2)}) %collective-permute-start.1) | collective-permute-done | bytes 1048608 | tf_op jit(solution)/shard_map/ppermute | solution.py:18
  130.1 2.3 %constant_dynamic-update-slice_fusion.3 = bf16[2048,1024]{1,0:T(8,128)(2,1)} fusion(bf16[2048,1024]{1,0:T(8,128)(2,1)} %constant_dynamic-update-slice_fusion.4, bf16[512,1024]{1,0:T(8,128)(2,1)} %collective-permute-done.1), kind=kLoop, calls=%fused_computation.30 | loop fusion | bytes 2097152
  132.5 0.8 constant_dynamic-update-slice_fusion.2
  133.3 0.8 constant_dynamic-update-slice_fusion.1
  134.1 2.3 %constant_dynamic-update-slice_fusion = bf16[2048,1024]{1,0:T(8,128)(2,1)} fusion(bf16[2048,1024]{1,0:T(8,128)(2,1)} %constant_dynamic-update-slice_fusion.1, bf16[512,1024]{1,0:T(8,128)(2,1)} %collective-permute-done.1), kind=kLoop, calls=%fused_computation.27 | loop fusion | bytes 2097152 | tf_op jit(solution)/shard_map/jit(_roll_dynamic)/concatenate | solution.py:22
  136.4 4.0 %fusion.12 = bf16[1024,256]{0,1:T(8,128)(2,1)S(1)} fusion(bf16[1,1024,1024]{2,1,0:T(8,128)(2,1)S(1)} %copy-done, bf16[2048,1024]{1,0:T(8,128)(2,1)} %constant_dynamic-update-slice_fusion, s32[]{:T(128)S(6)} %select_n.19, bf16[1,1024,1024]{2,1,0:T(8,128)(2,1)} %param.9, s32[]{:T(128)S(6)} %select_n.17), kind=kOutput, calls=%fused_computation.12 | convolution fusion | flops 1074266112 | bytes 5242888 | tf_op jit(solution)/shard_map/dot_general | solution.py:88
  140.4 0.2 copy.25
  140.6 11.7 %all_to_all.22 = bf16[2,4,128,256]{3,2,1,0:T(8,128)(2,1)S(1)} all-to-all(bf16[2,4,128,256]{3,2,1,0:T(8,128)(2,1)S(1)} %bitcast.64), channel_id=1, replica_groups=mesh['dp'=4,'half'=2,'own'=4] {'half'}, dimensions={0} | all-to-all | bytes 1048576 | tf_op jit(solution)/shard_map/all_to_all | solution.py:93
  152.3 18.8 %all_to_all.23 = bf16[2,4,128,256]{3,2,0,1:T(8,128)(2,1)S(1)} all-to-all(bf16[2,4,128,256]{3,2,0,1:T(8,128)(2,1)S(1)} %copy.23), channel_id=1, replica_groups=mesh['dp'=4,'half'=2,'own'=4] {'own'}, dimensions={1} | all-to-all | bytes 1048576 | tf_op jit(solution)/shard_map/all_to_all | solution.py:92
  171.2 0.3 copy.28
  171.5 0.4 convolution_convert_fusion
  171.8 0.8 copy.31
  (7 shorter events, 0.1 us)
Async XLA Ops:
  6.5 85.3 %copy-start = (bf16[1,1024,1024]{2,1,0:T(8,128)(2,1)S(1)}, bf16[1,1024,1024]{2,1,0:T(8,128)(2,1)}, u32[]{:S(2)}) copy-start(bf16[1,1024,1024]{2,1,0:T(8,128)(2,1)} %param.8) | copy-start | bytes 6291460
  6.5 34.1 %reduce-scatter.2.cloned.1.call-start = ((), (), s32[]{:S(2)}) async-start(), calls=%async_computation.5 | async-start | bytes 1966080 | tf_op jit(solution)/shard_map/reduce_scatter | solution.py:44
  7.3 84.5 %all-gather.2.cloned.1.call-start = ((), (), s32[]{:S(2)}) async-start(), calls=%async_computation.6 | async-start | bytes 2621440 | tf_op jit(solution)/shard_map/all_gather | solution.py:68
  52.8 39.0 %copy-start.1 = (bf16[1,256,1024]{2,1,0:T(8,128)(2,1)S(1)}, bf16[1,256,1024]{2,1,0:T(8,128)(2,1)}, u32[]{:S(2)}) copy-start(bf16[1,256,1024]{2,1,0:T(8,128)(2,1)} %param.11) | copy-start | bytes 1572868
  96.8 6.9 %collective-permute-start = (bf16[256,1024]{1,0:T(8,128)(2,1)S(1)}, bf16[256,1024]{1,0:T(8,128)(2,1)S(1)}, u32[]{:S(2)}, u32[]{:S(2)}) collective-permute-start(bf16[256,1024]{1,0:T(8,128)(2,1)S(1)} %get-tuple-element.6), channel_id=1, source_target_pairs={{0,24},{8,0},{16,8},{24,16},{1,25},{9,1},{17,9},{25,17},{2,26},{10... | collective-permute-start | bytes 1572872 | tf_op jit(solution)/shard_map/ppermute | solution.py:18
  104.8 25.4 %collective-permute-start.1 = (bf16[512,1024]{1,0:T(8,128)(2,1)}, bf16[512,1024]{1,0:T(8,128)(2,1)}, u32[]{:S(2)}, u32[]{:S(2)}) collective-permute-start(bf16[512,1024]{1,0:T(8,128)(2,1)} %pad_maximum_fusion), channel_id=1, source_target_pairs={{0,16},{8,24},{16,0},{24,8},{1,17},{9,25},{17,1},{25,9},{2,18},{10... | collective-permute-start | bytes 3145736 | tf_op jit(solution)/shard_map/ppermute | solution.py:18
Sparse Core Ops, SparseCore 0:
  9.9 30.7 reduce-scatter.1
  71.7 20.0 all-gather.1
